TPU v7x, 32 devices: a whole 2x2x4 slice. The times are simulated.
32 devices in a mesh: rep: 4 (over x, core), shard: 8 (over z, y).
Axes of the slice: x: 2, y: 2, z: 4, core: 2. Of those that a mesh axis runs over, the one named last changes fastest.
Arguments:
- dense_out: bfloat16 [4096, 128], P(('rep', 'shard')), may hold values from -0.75 to 0.75
- pooled: bfloat16 [4096, 26, 128], P(('rep', 'shard')), may hold values from -0.75 to 0.75
- top_weight: bfloat16 [479, 1024], replicated, may hold values from -0.25 to 0.25
- top_cotangent: bfloat16 [4096, 1024], P(('rep', 'shard')), may hold values from -3 to 3
- indices: int32 [4096, 26, 2], P(('rep', 'shard')), may hold values from 0 to 2047, as said below
Outputs:
- dense_grad: bfloat16 [4096, 128], P(('rep', 'shard'))
- top_grad: float32 [479, 1024], replicated
- bias_grad: float32 [1024], replicated
- table_grad: float32 [26, 2048, 128], P(None, 'shard')
Inputs may be any that keep to these rules, and one draw needn't show every extreme that they name: `indices`: rows r with r // 256 = s are held by shard s. For every device's 128 samples and every table, at most 16 of the device's lookups fall in any one block of 64 rows starting at a multiple of 64, and some such block holds exactly 16.
All inputs are finite; a program needn't handle non-finite values.
Results may differ from a plain program's by a relative error of at most 0.008.
Values may be sent and summed in bfloat16 or wider, within the bound.
A program may use at most 128 MiB of HBM per device.

v0:
```python
import jax
import jax.numpy as jnp
import numpy as np
from jax import lax
from jax.sharding import PartitionSpec as P

R_SHARD = 256


highest = lax.Precision.HIGHEST


def one_hot_sums(rows, keys, height):
    tables_here = rows.shape[0]
    flat_rows = rows.reshape(tables_here, -1, rows.shape[-1])
    flat_keys = keys.reshape(tables_here, -1)

    def per_table(member):
        table_rows, table_keys = member
        levels = lax.broadcasted_iota(jnp.int32, (height, table_keys.shape[0]), 0)
        matches = (levels == table_keys[None, :]).astype(jnp.bfloat16)
        return jnp.dot(matches, table_rows, preferred_element_type=jnp.float32)

    return lax.map(per_table, (flat_rows, flat_keys))


def pair_table(vectors):
    lower_i, lower_j = np.tril_indices(vectors, -1)
    select = np.zeros((vectors * vectors, lower_i.shape[0]), np.float32)
    select[lower_i * vectors + lower_j, np.arange(lower_i.shape[0])] = 1.0
    mirrored = np.zeros((lower_i.shape[0], vectors * vectors), np.float32)
    mirrored[np.arange(lower_i.shape[0]), lower_i * vectors + lower_j] = 1.0
    mirrored[np.arange(lower_i.shape[0]), lower_j * vectors + lower_i] = 1.0
    return (jnp.asarray(select), jnp.asarray(mirrored))


def on_device(dense_out, pooled, top_weight, top_cotangent, indices):
    samples = dense_out.shape[0]
    emb_width = dense_out.shape[1]
    tables = pooled.shape[1]
    lookups = indices.shape[2]
    replicas = lax.axis_size("rep")
    shards = lax.axis_size("shard")
    vectors = tables + 1
    select, mirrored = pair_table(vectors)
    stacked = jnp.concatenate([dense_out[:, None, :], pooled], axis=1)
    gram_matrix = jnp.einsum("bie,bje->bij", stacked, stacked, preferred_element_type=jnp.float32)
    gram_flat = gram_matrix.reshape(samples, vectors * vectors)
    pair_values = jnp.dot(
        gram_flat, select, precision=highest, preferred_element_type=jnp.float32
    ).astype(jnp.bfloat16)
    joined = jnp.concatenate([dense_out, pair_values], axis=1)
    grad_in = lax.dot_general(
        top_cotangent, top_weight, (((1,), (1,)), ((), ())), preferred_element_type=jnp.float32
    )
    top_part = lax.dot_general(
        joined, top_cotangent, (((0,), (0,)), ((), ())), preferred_element_type=jnp.float32
    )
    bias_part = jnp.sum(top_cotangent, axis=0, dtype=jnp.float32)
    pair_grad = grad_in[:, emb_width:]
    mirror = jnp.dot(
        pair_grad, mirrored, precision=highest, preferred_element_type=jnp.float32
    ).reshape(samples, vectors, vectors)
    mirror_high = mirror.astype(jnp.bfloat16)
    mirror_low = (mirror - mirror_high.astype(jnp.float32)).astype(jnp.bfloat16)
    vec_grad = jnp.einsum("bij,bje->bie", mirror_high, stacked, preferred_element_type=jnp.float32)
    vec_grad = vec_grad + jnp.einsum(
        "bij,bje->bie", mirror_low, stacked, preferred_element_type=jnp.float32
    )
    dense_grad = (grad_in[:, :emb_width] + vec_grad[:, 0]).astype(jnp.bfloat16)
    pooled_grad = vec_grad[:, 1:].astype(jnp.bfloat16)
    row_span = R_SHARD // replicas
    blocks = replicas * shards
    per_block = 2 * samples * lookups // blocks
    count_here = samples * lookups
    capacity = blocks * per_block
    by_table = jnp.transpose(indices, (1, 0, 2)).reshape(tables, count_here)
    lookup_rows = jnp.broadcast_to(
        jnp.transpose(pooled_grad, (1, 0, 2))[:, :, None, :], (tables, samples, lookups, emb_width)
    ).reshape(tables, count_here, emb_width)

    def place_table(member):
        table_keys, table_rows = member
        block_row = table_keys // row_span
        later = lax.broadcasted_iota(jnp.int32, (count_here, count_here), 0)
        sooner = lax.broadcasted_iota(jnp.int32, (count_here, count_here), 1)
        earlier = (block_row[None, :] == block_row[:, None]) & (sooner < later)
        slot_row = block_row * per_block + jnp.sum(earlier, axis=1, dtype=jnp.int32)
        levels = lax.broadcasted_iota(jnp.int32, (capacity, count_here), 0)
        placed = levels == slot_row[None, :]
        rows_out = jnp.dot(
            placed.astype(jnp.bfloat16), table_rows, preferred_element_type=jnp.float32
        ).astype(jnp.bfloat16)
        keys_out = (
            jnp.sum(
                jnp.where(placed, (table_keys % R_SHARD + 1)[None, :], 0), axis=1, dtype=jnp.int32
            )
            - 1
        )
        return (rows_out, keys_out)

    send_rows, send_keys = lax.map(place_table, (by_table, lookup_rows))
    top_grad, bias_grad = lax.psum((top_part, bias_part), ("rep", "shard"))
    grouped_rows = send_rows.reshape(tables, shards, replicas * per_block, emb_width)
    grouped_keys = send_keys.reshape(tables, shards, replicas * per_block)
    partial_value = one_hot_sums(
        lax.all_to_all(grouped_rows, "shard", split_axis=1, concat_axis=1, tiled=True),
        lax.all_to_all(grouped_keys, "shard", split_axis=1, concat_axis=1, tiled=True),
        R_SHARD,
    )
    table_grad = lax.psum(partial_value, "rep")
    return (dense_grad, top_grad, bias_grad, table_grad)


def solution(mesh):
    return jax.shard_map(
        on_device,
        mesh=mesh,
        in_specs=(
            P(("rep", "shard"), None),
            P(("rep", "shard"), None, None),
            P(),
            P(("rep", "shard"), None),
            P(("rep", "shard"), None, None),
        ),
        out_specs=(P(("rep", "shard"), None), P(), P(), P(None, "shard", None)),
        check_vma=False,
    )
```

profile of v0, /device:TPU:0, one launch (start us, length us, event | category | flops | bytes accessed | tf_op | source)
XLA Modules:
  0.0 386.4 jit_solution(17738884548787175198)
XLA Ops:
  9.8 2.0 fusion.17
  17.7 2.8 copy.78
  20.6 2.4 copy.77
  24.8 2.9 copy.79
  27.7 2.2 add.78
  34.0 2.4 broadcast_in_dim.67
  36.3 57.8 %while.25 = (s32[]{:T(128)}, bf16[26,512,128]{2,1,0:T(8,128)(2,1)}, s32[26,512]{1,0:T(8,128)S(1)}, s32[26,256]{1,0:T(8,128)S(1)}, bf16[26,256,128]{2,1,0:T(8,128)(2,1)}, /*index=5*/s32[]{:T(128)}, s32[]{:T(128)}) while((s32[]{:T(128)}, bf16[26,512,128]{2,1,0:T(8,128)(2,1)}, s32[26,512]{1,0:T(8,128)S(1)}, s32[26,256]{1,0:T(8,128)S(1)}, ...), condition=%wide.region_6.7_spmd, body=%wide.region_3.6_spmd.sunk | while | flops 34486784 | bytes 224341 | solution.py:102
  95.0 7.3 %all-to-all-start = ((s32[8,1,1664]{2,1,0:T(1,128)}), s32[8,1,1664]{2,1,0:T(1,128)S(1)}, u32[]{:S(2)}, u32[]{:S(2)}) async-start(s32[8,1,1664]{2,1,0:T(1,128)} %reshape.98), calls=%async_computation | async-start | bytes 106496 | tf_op jit(solution)/shard_map/all_to_all | solution.py:108
  102.3 4.8 %copy.87 = bf16[26,8,64,128]{3,2,0,1:T(8,128)(2,1)} copy(bf16[26,8,64,128]{3,2,1,0:T(8,128)(2,1)} %bitcast.71) | data formatting | bytes 6815744 | tf_op jit(solution)/shard_map/reshape | solution.py:104
  107.1 2.0 all-to-all-done
  109.1 4.5 %all-to-all-start.1 = ((bf16[26,8,64,128]{3,2,0,1:T(8,128)(2,1)}), bf16[26,8,64,128]{3,2,0,1:T(8,128)(2,1)}, u32[]{:S(2)}, u32[]{:S(2)}) async-start(bf16[26,8,64,128]{3,2,0,1:T(8,128)(2,1)} %copy.87), calls=%async_computation.1 | async-start | bytes 6815744 | tf_op jit(solution)/shard_map/all_to_all | solution.py:107
  114.5 2.0 fusion.14
  116.5 2.9 reshape.97
  119.4 2.0 convolution_convert_fusion.1
  124.8 73.4 %all-to-all-done.1 = bf16[26,8,64,128]{3,2,0,1:T(8,128)(2,1)} async-done(((bf16[26,8,64,128]{3,2,0,1:T(8,128)(2,1)}), bf16[26,8,64,128]{3,2,0,1:T(8,128)(2,1)}, u32[]{:S(2)}, u32[]{:S(2)}) %all-to-all-start.1) | async-done | bytes 3407904 | tf_op jit(solution)/shard_map/all_to_all | solution.py:107
  198.2 4.8 %copy.88 = bf16[26,8,64,128]{3,2,1,0:T(8,128)(2,1)} copy(bf16[26,8,64,128]{3,2,0,1:T(8,128)(2,1)} %all-to-all-done.1) | data formatting | bytes 6815744 | tf_op jit(solution)/shard_map/all_to_all | solution.py:107
  203.0 47.0 %while.26 = (s32[]{:T(128)}, f32[26,256,128]{2,1,0:T(8,128)}, s32[26,512]{1,0:T(8,128)S(1)}, bf16[26,512,128]{2,1,0:T(8,128)(2,1)}, s32[]{:T(128)}) while((s32[]{:T(128)}, f32[26,256,128]{2,1,0:T(8,128)}, s32[26,512]{1,0:T(8,128)S(1)}, bf16[26,512,128]{2,1,0:T(8,128)(2,1)}, s32[]{:T(128)}) %tuple.72), condition=%wide.region_8.9_spmd, body=%wide.region_7.8_spmd.sunk | while | flops 33685504 | bytes 269377 | solution.py:24
  204.8 1.8 fusion.47
  208.4 1.8 fusion.47
  219.3 1.8 fusion.47
  222.9 1.8 fusion.47
  224.7 1.8 fusion.47
  226.5 1.8 fusion.47
  228.3 1.8 fusion.47
  230.1 1.8 fusion.47
  235.5 1.8 fusion.47
  237.3 1.8 fusion.47
  244.6 1.8 fusion.47
  251.6 38.0 %psum.22 = f32[1024]{0:T(1024)} all-reduce(f32[1024]{0:T(1024)S(1)} %convert_reduce_fusion.1), channel_id=1, replica_groups=mesh['rep'=4,'shard'=8] {'rep','shard'}, use_global_device_ids=true, to_apply=%region_2.3 | all-reduce | flops 1024 | bytes 8192 | tf_op jit(solution)/shard_map/psum | solution.py:103
  289.6 10.4 %all-reduce.3.cloned.1.call-done = f32[479,1024]{1,0:T(8,128)} async-done(((f32[479,1024]{1,0:T(8,128)}), f32[479,1024]{1,0:T(8,128)}) %all-reduce.3.cloned.1.call-update) | async-done | bytes 1962000 | tf_op jit(solution)/shard_map/psum | solution.py:103
  300.1 74.5 %all-reduce.5.cloned.1.call-done = f32[26,256,128]{2,1,0:T(8,128)} async-done(((f32[26,256,128]{2,1,0:T(8,128)}), f32[26,256,128]{2,1,0:T(8,128)}) %all-reduce.5.cloned.1.call-update) | async-done | bytes 3407888 | tf_op jit(solution)/shard_map/psum | solution.py:111
  374.6 3.2 copy.115
  (326 shorter events, 106.8 us)
Async XLA Ops:
  7.2 1.2 copy-start
  7.2 2.6 copy-start.5
  11.8 4.1 %copy-start.7 = (bf16[128,128]{1,0:T(8,128)(2,1)S(1)}, bf16[128,128]{1,0:T(8,128)(2,1)}, u32[]{:S(2)}) copy-start(bf16[128,128]{1,0:T(8,128)(2,1)} %param.11) | copy-start | bytes 98308
  29.9 1.3 copy-start.1
  31.1 2.6 copy-start.8
  95.0 14.1 %all-to-all-start = ((s32[8,1,1664]{2,1,0:T(1,128)}), s32[8,1,1664]{2,1,0:T(1,128)S(1)}, u32[]{:S(2)}, u32[]{:S(2)}) async-start(s32[8,1,1664]{2,1,0:T(1,128)} %reshape.98), calls=%async_computation | async-start | bytes 106496 | tf_op jit(solution)/shard_map/all_to_all | solution.py:108
  109.1 89.1 %all-to-all-start.1 = ((bf16[26,8,64,128]{3,2,0,1:T(8,128)(2,1)}), bf16[26,8,64,128]{3,2,0,1:T(8,128)(2,1)}, u32[]{:S(2)}, u32[]{:S(2)}) async-start(bf16[26,8,64,128]{3,2,0,1:T(8,128)(2,1)} %copy.87), calls=%async_computation.1 | async-start | bytes 6815744 | tf_op jit(solution)/shard_map/all_to_all | solution.py:107
  113.6 186.5 %all-reduce.3.cloned.1.call-start = ((), (), s32[]{:S(2)}) async-start(), calls=%async_computation.2 | async-start | bytes 3932160 | tf_op jit(solution)/shard_map/psum | solution.py:103
  114.5 4.9 %copy-start.4 = (f32[729,351]{1,0:T(8,128)S(1)}, f32[729,351]{1,0:T(8,128)}, u32[]{:S(2)}) copy-start(f32[729,351]{1,0:T(8,128)} %constant.104.clone) | copy-start | bytes 3070552
  116.5 4.9 %copy-start.3 = (bf16[128,1024]{1,0:T(8,128)(2,1)S(1)}, bf16[128,1024]{1,0:T(8,128)(2,1)}, u32[]{:S(2)}) copy-start(bf16[128,1024]{1,0:T(8,128)(2,1)} %param.14) | copy-start | bytes 786436
  116.5 4.9 %copy-start.6 = (bf16[128,128]{0,1:T(8,128)(2,1)S(1)}, bf16[128,128]{0,1:T(8,128)(2,1)}, u32[]{:S(2)}) copy-start(bf16[128,128]{0,1:T(8,128)(2,1)} %copy.81) | copy-start | bytes 98308
  123.2 251.4 %all-reduce.5.cloned.1.call-start = ((), (), s32[]{:S(2)}) async-start(), calls=%async_computation.3 | async-start | bytes 6815744 | tf_op jit(solution)/shard_map/psum | solution.py:111
  374.6 3.2 copy-start.2
Sparse Core Ops, SparseCore 0:
  123.3 176.7 all-reduce.2
  303.0 71.5 all-reduce.4
where the time goes:
time: 389 us; the launch traced here: 386 us
  waiting for transfers between devices  160 us (41%)
  matrix products  105 us (27%)
  local copies, waits for them, and re-layouts  41.3 us (11%)
  blocking collectives  38 us (10%)
  other arithmetic  14.6 us (4%)
  between operations  14.3 us (4%)
  starting transfers between devices  12 us (3%)
    psum x1, waiting for transfers between devices, on_device(): table_grad = lax.psum(partial_value, 'rep')  74.5 us
    all_to_all x1, waiting for transfers between devices, on_device(): lax.all_to_all(grouped_rows, 'shard', split_axis=1, concat_axis=1, tiled=...  73.4 us
    dot_general x26, matrix products, per_table(): return jnp.dot(matches, table_rows, preferred_element_type=jnp.float32)  46.8 us
    dot_general x26, matrix products, place_table(): jnp.dot(placed.astype(jnp.bfloat16), table_rows, preferred_element_type=j...  45.3 us
    psum x1, blocking collectives, on_device(): top_grad, bias_grad = lax.psum((top_part, bias_part), ('rep', 'shard'))  38 us
    unnamed x25, local copies, waits for them, and re-layouts  11.4 us
    psum x1, waiting for transfers between devices, on_device(): top_grad, bias_grad = lax.psum((top_part, bias_part), ('rep', 'shard'))  10.4 us
  transfers between devices with their start and end apart: 4, of which 4 were waited for; matrix products, arithmetic and copies ran while one was open for 18% of the time, Pallas kernels for 0%

commit v1 on v0

v1 whole, which is shorter than its diff:
```python
import functools

import jax
import jax.numpy as jnp
from jax import lax
from jax.experimental import pallas as pl
from jax.experimental.pallas import tpu as pltpu
from jax.sharding import PartitionSpec as P

PAIR = 2
MESH = pl.DeviceIdType.MESH
VMEM = pl.BlockSpec(memory_space=pltpu.VMEM)
f32, bf16 = jnp.float32, jnp.bfloat16


def cdiv(a, b):
    return -(-a // b)


def local_kernel(nv, group, chunk, dense, pooled, weight, cot, dense_grad, rows_out, top_out, v, gram, mir, joined, grads, vg):
    emb, samples = v.shape[1], v.shape[2]
    features = weight.shape[0]
    v[0] = dense[...].astype(f32).T

    def load(t, _):
        v[t + 1] = pooled[t].astype(f32).T
        return 0

    lax.fori_loop(0, nv - 1, load, 0)
    grads[pl.ds(0, features), :] = lax.dot_general(
        weight[...], cot[...], (((1,), (1,)), ((), ())), preferred_element_type=f32
    )
    for start in range(0, nv, group):
        js = range(start, min(start + group, nv))

        def one(i, _, js=js):
            for j in js:
                gram[i, pl.ds(j, 1), :] = jnp.sum(v[i] * v[j], axis=0, keepdims=True)
            return 0

        lax.fori_loop(start + 1, nv, one, 0)
    joined[...] = jnp.zeros_like(joined)
    joined[pl.ds(0, emb), :] = v[0]
    mir[...] = jnp.zeros_like(mir)
    for i in range(1, nv):
        base = emb + i * (i - 1) // 2
        joined[pl.ds(base, i), :] = gram[i, pl.ds(0, i), :]
        mir[i, pl.ds(0, i), :] = grads[pl.ds(base, i), :]
        for j in range(i):
            mir[j, pl.ds(i, 1), :] = grads[pl.ds(base + j, 1), :]
    joined[pl.ds(features, 1), :] = jnp.ones((1, samples), f32)
    groups, width = top_out.shape[0], top_out.shape[2]
    left = joined[...].astype(bf16)
    for r in range(groups):
        top_out[r] = jnp.dot(
            left, cot[:, pl.ds(r * width, width)], preferred_element_type=f32
        ).astype(bf16)

    def part(c, _):
        where = pl.ds(pl.multiple_of(c * chunk, chunk), chunk)
        for start in range(0, nv, group):
            items = range(start, min(start + group, nv))

            def add(j, accs):
                vj = v[j, where, :]
                return tuple(a + vj * mir[j, pl.ds(i, 1), :] for a, i in zip(accs, items))

            accs = lax.fori_loop(
                0, nv, add, tuple(jnp.zeros((chunk, samples), f32) for _ in items)
            )
            for a, i in zip(accs, items):
                vg[i, where, :] = a
        return 0

    lax.fori_loop(0, emb // chunk, part, 0)
    dense_grad[...] = (grads[pl.ds(0, emb), :] + vg[0]).T.astype(bf16)

    def store(t, _):
        rows_out[t] = vg[t + 1].T.astype(bf16)
        return 0

    lax.fori_loop(0, nv - 1, store, 0)
    for t in range(nv - 1, rows_out.shape[0]):
        rows_out[t] = jnp.zeros_like(rows_out[t])


def comm_kernel(
    R, S, lookups, rows_in, keys_in, top_in, tab_out, top_out,
    rows, keys, part, prcv, own, fin, trcv, tsum, tred, tfin, tgat,
    s_rows, r_rows, s_keys, r_keys, s_top, r_top, s_yrow, r_yrow, s_ykey, r_ykey,
    s_part, r_part, s_fin, r_fin, s_t2, r_t2, s_t3, r_t3, s_t4, r_t4, l_sem,
):
    q, s = lax.axis_index("rep"), lax.axis_index("shard")
    Z = S // PAIR
    y, z = s % PAIR, s // PAIR
    mate = z * PAIR + (1 - y)
    T, span = part.shape[1], part.shape[2]
    B = rows.shape[3]
    chunk_rows = tgat.shape[1]

    def copy(src, dst, ssem, rsem, rep, shard):
        return pltpu.make_async_remote_copy(
            src_ref=src, dst_ref=dst, send_sem=ssem, recv_sem=rsem,
            device_id=(rep, shard), device_id_type=MESH,
        )

    barrier = pltpu.get_barrier_semaphore()
    for k in range(1, R):
        pl.semaphore_signal(barrier, inc=1, device_id=((q + k) % R, s), device_id_type=MESH)

    def greet(k, _):
        pl.semaphore_signal(barrier, inc=1, device_id=(q, (s + k) % S), device_id_type=MESH)
        return 0

    lax.fori_loop(1, S, greet, 0)
    pl.semaphore_wait(barrier, R - 1 + S - 1)

    def rep_copies(k):
        to = (q + k) % R
        return (
            copy(rows_in.at[to], rows.at[y, q], s_rows.at[k - 1], r_rows.at[k - 1], to, s),
            copy(keys_in.at[to], keys.at[y, q], s_keys.at[k - 1], r_keys.at[k - 1], to, s),
        )

    def top_copy(k):
        to = (q + k) % R
        return copy(top_in.at[to], trcv.at[k - 1], s_top.at[k - 1], r_top.at[k - 1], to, s)

    for k in range(1, R):
        for c in rep_copies(k):
            c.start()
    mine = pltpu.make_async_copy(rows_in.at[q], rows.at[y, q], l_sem.at[0])
    mine.start()
    mine_keys = pltpu.make_async_copy(keys_in.at[q], keys.at[y, q], l_sem.at[1])
    mine_keys.start()
    for k in range(1, R):
        top_copy(k).start()
    mine.wait()
    mine_keys.wait()

    def pair_copies(k):
        r = (q + R - k) % R
        return (
            copy(rows.at[y, r], rows.at[y, r], s_yrow.at[k], r_yrow.at[k], q, mate),
            copy(keys.at[y, r], keys.at[y, r], s_ykey.at[k], r_ykey.at[k], q, mate),
        )

    for c in pair_copies(0):
        c.start()
    for k in range(1, R):
        for c in rep_copies(k):
            c.wait_recv()
        for c in pair_copies(k):
            c.start()

    for k in range(1, R):
        top_copy(k).wait_recv()
    total = top_in[q].astype(f32)
    for k in range(1, R):
        total = total + trcv[k - 1].astype(f32)
    tsum[...] = total.astype(bf16).reshape(tsum.shape)

    def t2_copy(k):
        to = (s + k) % S
        return copy(tsum.at[to], tred.at[k - 1], s_t2.at[k - 1], r_t2.at[k - 1], q, to)

    def t3_copy(k):
        to = (s + k) % S
        return copy(tfin, tgat.at[s], s_t3.at[k - 1], r_t3.at[k - 1], q, to)

    def each(n, f):
        def step(k, _):
            f(k)
            return 0

        lax.fori_loop(1, n, step, 0)

    each(S, lambda k: t2_copy(k).start())

    for k in range(R):
        for c in pair_copies(k):
            c.wait_recv()

    levels = lax.broadcasted_iota(jnp.int32, (span, B), 0)

    def partial_of(t, shard):
        acc = jnp.zeros((span, rows.shape[4]), f32)
        for side in range(PAIR):
            for r in range(R):
                hits = None
                for l in range(lookups):
                    key = keys[side, r, pl.ds(t * lookups + l, 1), :] - shard * span
                    hit = jnp.where(levels == key, 1.0, 0.0)
                    hits = hit if hits is None else hits + hit
                acc = acc + jnp.dot(hits.astype(bf16), rows[side, r, t], preferred_element_type=f32)
        return acc

    def part_copy(k):
        to = ((z + k) % Z) * PAIR + y
        return copy(part.at[k - 1], prcv.at[k - 1], s_part.at[k - 1], r_part.at[k - 1], q, to)

    def send_part(k):
        to = ((z + k) % Z) * PAIR + y

        def table(t, _):
            part[k - 1, t] = partial_of(t, to).astype(bf16)
            return 0

        lax.fori_loop(0, T, table, 0)
        part_copy(k).start()

    each(Z, send_part)

    each(S, lambda k: t2_copy(k).wait_recv())
    tfin[...] = lax.fori_loop(
        1, S, lambda k, a: a + tred[k - 1].astype(f32), tsum[s].astype(f32)
    ).astype(bf16)
    each(S, lambda k: t3_copy(k).start())

    def own_table(t, _):
        own[t] = partial_of(t, s)
        return 0

    lax.fori_loop(0, T, own_table, 0)
    tgat[s] = tfin[...]
    each(S, lambda k: t3_copy(k).wait_recv())

    def t4_copy(k):
        to = (q + k) % R
        return copy(tgat, top_out.at[q], s_t4.at[k - 1], r_t4.at[k - 1], to, s)

    def fin_copy(k):
        to = (q + k) % R
        return copy(fin, tab_out.at[q], s_fin.at[k - 1], r_fin.at[k - 1], to, s)

    for k in range(1, R):
        t4_copy(k).start()
    each(Z, lambda k: part_copy(k).wait_recv())

    def finish(t, _):
        fin[t] = lax.fori_loop(
            1, Z, lambda k, a: a + prcv[k - 1, t].astype(f32), own[t]
        ).astype(bf16)
        return 0

    lax.fori_loop(0, T, finish, 0)
    for k in range(1, R):
        fin_copy(k).start()
    top_out[q] = tgat[...]
    tab_out[q] = fin[...]
    for k in range(1, R):
        for c in rep_copies(k):
            c.wait_send()
        top_copy(k).wait_send()
    for k in range(R):
        for c in pair_copies(k):
            c.wait_send()
    each(S, lambda k: t2_copy(k).wait_send())
    each(S, lambda k: t3_copy(k).wait_send())
    each(Z, lambda k: part_copy(k).wait_send())
    for k in range(1, R):
        t4_copy(k).wait()
        fin_copy(k).wait()


def on_device(span, R, S, dense_out, pooled, top_weight, top_cotangent, indices):
    samples, emb = dense_out.shape
    tables, lookups = pooled.shape[1], indices.shape[2]
    nv = tables + 1
    features, hidden = top_weight.shape
    T = cdiv(tables, R)
    chunk_rows = cdiv(features + 1, 16 * S) * 16
    height = chunk_rows * S
    width = hidden // R
    pad_v = cdiv(nv, 8) * 8
    dense_grad, rows, top = pl.pallas_call(
        functools.partial(local_kernel, nv, 9, 32),
        out_shape=(
            jax.ShapeDtypeStruct((samples, emb), bf16),
            jax.ShapeDtypeStruct((R * T, samples, emb), bf16),
            jax.ShapeDtypeStruct((R, height, width), bf16),
        ),
        in_specs=[VMEM] * 4,
        out_specs=(VMEM,) * 3,
        scratch_shapes=[
            pltpu.VMEM((nv, emb, samples), f32),
            pltpu.VMEM((nv, pad_v, samples), f32),
            pltpu.VMEM((nv, pad_v, samples), f32),
            pltpu.VMEM((height, samples), f32),
            pltpu.VMEM((cdiv(features, 8) * 8, samples), f32),
            pltpu.VMEM((nv, emb, samples), f32),
        ],
        compiler_params=pltpu.CompilerParams(vmem_limit_bytes=48 << 20),
        name="local_math",
    )(dense_out, jnp.transpose(pooled, (1, 0, 2)), top_weight, top_cotangent)

    keys = jnp.transpose(indices, (1, 2, 0))
    keys = jnp.pad(keys, ((0, R * T - tables), (0, 0), (0, 0)), constant_values=-1)
    keys = keys.reshape(R, T * lookups, samples)
    key_rows = cdiv(T * lookups, 8) * 8
    keys = jnp.pad(keys, ((0, 0), (0, key_rows - T * lookups), (0, 0)), constant_values=-1)

    Z = S // PAIR
    dma = pltpu.SemaphoreType.DMA
    table_all, top_all = pl.pallas_call(
        functools.partial(comm_kernel, R, S, lookups),
        out_shape=(
            jax.ShapeDtypeStruct((R, T, span, emb), bf16),
            jax.ShapeDtypeStruct((R, S, chunk_rows, width), bf16),
        ),
        in_specs=[VMEM] * 3,
        out_specs=(VMEM,) * 2,
        scratch_shapes=[
            pltpu.VMEM((PAIR, R, T, samples, emb), bf16),
            pltpu.VMEM((PAIR, R, key_rows, samples), jnp.int32),
            pltpu.VMEM((Z - 1, T, span, emb), bf16),
            pltpu.VMEM((Z - 1, T, span, emb), bf16),
            pltpu.VMEM((T, span, emb), f32),
            pltpu.VMEM((T, span, emb), bf16),
            pltpu.VMEM((R - 1, S, chunk_rows, width), bf16),
            pltpu.VMEM((S, chunk_rows, width), bf16),
            pltpu.VMEM((S - 1, chunk_rows, width), bf16),
            pltpu.VMEM((chunk_rows, width), bf16),
            pltpu.VMEM((S, chunk_rows, width), bf16),
            dma((R - 1,)), dma((R - 1,)), dma((R - 1,)), dma((R - 1,)), dma((R - 1,)), dma((R - 1,)),
            dma((R,)), dma((R,)), dma((R,)), dma((R,)),
            dma((Z - 1,)), dma((Z - 1,)), dma((R - 1,)), dma((R - 1,)),
            dma((S - 1,)), dma((S - 1,)), dma((S - 1,)), dma((S - 1,)),
            dma((R - 1,)), dma((R - 1,)), dma((2,)),
        ],
        compiler_params=pltpu.CompilerParams(
            collective_id=0, has_side_effects=True, vmem_limit_bytes=60 << 20
        ),
        name="exchange",
    )(rows.reshape(R, T, samples, emb), keys, top.reshape(R, S, chunk_rows, width))
    table_grad = table_all.reshape(R * T, span, emb)[:tables].astype(f32)
    whole = jnp.transpose(top_all.reshape(R, height, width), (1, 0, 2)).reshape(height, hidden)
    top_grad = whole[:features].astype(f32)
    bias_grad = whole[features].astype(f32)
    return dense_grad, top_grad, bias_grad, table_grad


ROWS_PER_SHARD = 256


def solution(mesh):
    return jax.shard_map(
        functools.partial(on_device, ROWS_PER_SHARD, mesh.shape["rep"], mesh.shape["shard"]),
        mesh=mesh,
        in_specs=(
            P(("rep", "shard"), None),
            P(("rep", "shard"), None, None),
            P(),
            P(("rep", "shard"), None),
            P(("rep", "shard"), None, None),
        ),
        out_specs=(P(("rep", "shard"), None), P(), P(), P(None, "shard", None)),
        check_vma=False,
    )
```

time: 389 us -> 147 us (0.38)
  waiting for transfers between devices: 160 us -> 0 us
  Pallas kernels: 0 us -> 129 us
  matrix products: 105 us -> 0 us
  blocking collectives: 38 us -> 0 us
  local copies, waits for them, and re-layouts: 41.3 us -> 10.7 us
  between operations: 14.3 us -> 0.69 us
  starting transfers between devices: 12 us -> 0 us
  other arithmetic: 14.6 us -> 4.81 us
    pallas_call x0 -> x2, Pallas kernels: none -> 129 us  [the longest x1 112 us: on_device(): pl.pallas_call(functools.partial(comm_kernel, R, S, lookups), out_shape=(...]
    dot_general x59 -> x0, matrix products: 105 us -> none  [the longest x26 46.8 us: per_table(): return jnp.dot(matches, table_rows, preferred_element_type=jnp.float32)]
    psum x2 -> x0, waiting for transfers between devices: 85 us -> none  [the longest x1 74.5 us: on_device(): table_grad = lax.psum(partial_value, 'rep')]
    all_to_all x2 -> x0, waiting for transfers between devices: 75.4 us -> none  [the longest x1 73.4 us: on_device(): lax.all_to_all(grouped_rows, 'shard', split_axis=1, concat_axis=1, tiled=...]
    psum x1 -> x0, blocking collectives: 38 us -> none  [on_device(): top_grad, bias_grad = lax.psum((top_part, bias_part), ('rep', 'shard'))]
    all_to_all x2 -> x0, starting transfers between devices: 11.8 us -> none  [the longest x1 7.31 us: on_device(): lax.all_to_all(grouped_keys, 'shard', split_axis=1, concat_axis=1, tiled=...]
    reduce_sum x53 -> x0, other arithmetic: 8.66 us -> none  [the longest x26 4.72 us: place_table(): slot_row = block_row * per_block + jnp.sum(earlier, axis=1, dtype=jnp.int32)]
    reshape x6 -> x1, local copies, waits for them, and re-layouts: 7.87 us -> 0.02 us  [on_device(): keys = keys.reshape(R, T * lookups, samples)]
  transfers between devices with their start and end apart: 4 -> 0, of which waited for: 4 -> 0; matrix products, arithmetic and copies ran while one was open for 18% -> 0% of each run, Pallas kernels for 0% -> 0%
where the time goes in v1:
time: 147 us; the launch traced here: 145 us
  Pallas kernels  129 us (88%)
  local copies, waits for them, and re-layouts  10.7 us (7%)
  other arithmetic  4.81 us (3%)
    pallas_call x1, Pallas kernels, on_device(): pl.pallas_call(functools.partial(comm_kernel, R, S, lookups), out_shape=(...  112 us
    pallas_call x1, Pallas kernels, on_device(): pl.pallas_call(functools.partial(local_kernel, nv, 9, 32), out_shape=(jax...  16.7 us
    unnamed x16, local copies, waits for them, and re-layouts  8.02 us

profile of v1, /device:TPU:0, one launch (start us, length us, event | category | flops | bytes accessed | tf_op | source)
XLA Modules:
  0.0 145.0 jit_solution(17926939170937529817)
XLA Ops:
  0.6 0.8 pad.8
  1.4 0.6 pad.9.keys_in
  2.0 0.0 copy-start.1
  2.0 1.2 copy-done.1
  3.2 0.0 copy-start.3
  3.2 1.2 copy-done.3
  4.4 0.0 copy-start.4
  4.4 0.9 copy-done.4
  5.3 0.0 copy-start.5
  5.3 0.8 copy-done.5
  6.1 16.7 %local_math.1 = (bf16[128,128]{1,0:T(8,128)(2,1)}, bf16[28,128,128]{2,1,0:T(8,128)(2,1)S(1)}, bf16[4,512,256]{2,1,0:T(8,128)(2,1)S(1)}) custom-call(bf16[128,128]{1,0:T(8,128)(2,1)S(1)} %copy-done.5, bf16[26,128,128]{2,1,0:T(8,128)(2,1)S(1)} %bitcast.14, bf16[479,1024]{1,0:T(8,128)(2,1)S(1)} %copy-done.1, bf16[128,1024]{1,0:T(8,128)(2,1)S(1)} %copy-done.4), custom_call_target="tpu_custom_call" | custom-call | tf_op jit(solution)/shard_map/local_math/pallas_call | solution.py:276
  22.8 0.0 copy-start
  22.8 1.0 copy-done
  23.8 0.0 copy-start.2
  23.8 0.9 copy-done.2
  24.7 112.1 %exchange.1 = (bf16[4,7,256,128]{3,2,1,0:T(8,128)(2,1)}, bf16[4,8,64,256]{3,2,1,0:T(8,128)(2,1)}) custom-call(bf16[4,7,128,128]{3,2,1,0:T(8,128)(2,1)} %bitcast.13, s32[4,16,128]{2,1,0:T(8,128)} %pad.9.keys_in, bf16[4,8,64,256]{3,2,1,0:T(8,128)(2,1)} %bitcast.12), custom_call_target="tpu_custom_call" | custom-call | tf_op jit(solution)/shard_map/exchange/pallas_call | solution.py:305
  136.8 1.3 slice_convert_fusion.2
  138.1 1.4 slice_convert_fusion.1
  139.5 1.3 copy.10
  140.8 0.3 pad.10
  141.1 0.0 copy-start.6
  141.1 1.7 %copy.11 = f32[60,8,4,256]{3,1,2,0:T(8,128)} copy(f32[60,8,4,256]{3,2,1,0:T(4,128)S(1)} %bitcast.15) | data formatting | bytes 3932160
  142.8 0.0 copy-done.6
  142.9 2.1 %slice_convert_fusion = f32[26,256,128]{2,1,0:T(8,128)} fusion(bf16[28,256,128]{2,1,0:T(8,128)(2,1)S(1)} %bitcast.17), kind=kLoop, calls=%fused_computation | loop fusion | flops 851968 | bytes 5111808 | tf_op jit(solution)/shard_map/convert_element_type | solution.py:336
  (1 shorter events, 0.0 us)
Async XLA Ops:
  2.0 1.2 copy-start.1
  3.2 1.2 copy-start.3
  4.4 0.9 copy-start.4
  5.3 0.8 copy-start.5
  22.8 1.0 copy-start
  23.8 0.9 copy-start.2
  141.1 1.7 %copy-start.6 = (bf16[4,7,256,128]{3,2,1,0:T(8,128)(2,1)S(1)}, bf16[4,7,256,128]{3,2,1,0:T(8,128)(2,1)}, u32[]{:S(2)}) copy-start(bf16[4,7,256,128]{3,2,1,0:T(8,128)(2,1)} %get-tuple-element.13) | copy-start | bytes 5505028

commit v2 on v1

--- a/solution.py
+++ b/solution.py
@@ -8,6 +8,7 @@
 from jax.sharding import PartitionSpec as P
 
 PAIR = 2
+CORES = 2
 MESH = pl.DeviceIdType.MESH
 VMEM = pl.BlockSpec(memory_space=pltpu.VMEM)
 f32, bf16 = jnp.float32, jnp.bfloat16
@@ -86,17 +87,19 @@
 
 def comm_kernel(
     R, S, lookups, rows_in, keys_in, top_in, tab_out, top_out,
-    rows, keys, part, prcv, own, fin, trcv, tsum, tred, tfin, tgat,
+    rows, keys, part, prcv, own, trcv, tsum, tred, tfin,
     s_rows, r_rows, s_keys, r_keys, s_top, r_top, s_yrow, r_yrow, s_ykey, r_ykey,
-    s_part, r_part, s_fin, r_fin, s_t2, r_t2, s_t3, r_t3, s_t4, r_t4, l_sem,
+    s_part, r_part, s_fin, r_fin, s_fwd, r_fwd, s_t2, r_t2, s_t3, r_t3,
+    s_t4, r_t4, s_t5, r_t5, l_rows, l_keys,
 ):
     q, s = lax.axis_index("rep"), lax.axis_index("shard")
-    Z = S // PAIR
+    Z, X = S // PAIR, R // CORES
     y, z = s % PAIR, s // PAIR
     mate = z * PAIR + (1 - y)
-    T, span = part.shape[1], part.shape[2]
+    core = q % CORES
+    twin = q - core + (1 - core)
+    T, span = own.shape[0], own.shape[1]
     B = rows.shape[3]
-    chunk_rows = tgat.shape[1]
 
     def copy(src, dst, ssem, rsem, rep, shard):
         return pltpu.make_async_remote_copy(
@@ -104,82 +107,60 @@
             device_id=(rep, shard), device_id_type=MESH,
         )
 
+    def each(start, stop, f):
+        def step(k, _):
+            f(k)
+            return 0
+
+        lax.fori_loop(start, stop, step, 0)
+
     barrier = pltpu.get_barrier_semaphore()
     for k in range(1, R):
         pl.semaphore_signal(barrier, inc=1, device_id=((q + k) % R, s), device_id_type=MESH)
-
-    def greet(k, _):
-        pl.semaphore_signal(barrier, inc=1, device_id=(q, (s + k) % S), device_id_type=MESH)
-        return 0
-
-    lax.fori_loop(1, S, greet, 0)
+    each(1, S, lambda k: pl.semaphore_signal(
+        barrier, inc=1, device_id=(q, (s + k) % S), device_id_type=MESH))
     pl.semaphore_wait(barrier, R - 1 + S - 1)
 
-    def rep_copies(k):
+    def row_copy(t, k):
         to = (q + k) % R
-        return (
-            copy(rows_in.at[to], rows.at[y, q], s_rows.at[k - 1], r_rows.at[k - 1], to, s),
-            copy(keys_in.at[to], keys.at[y, q], s_keys.at[k - 1], r_keys.at[k - 1], to, s),
-        )
+        return copy(rows_in.at[to, t], rows.at[y, t, q], s_rows.at[t, k - 1], r_rows.at[t, k - 1], to, s)
+
+    def own_row_copy(t):
+        return pltpu.make_async_copy(rows_in.at[q, t], rows.at[y, t, q], l_rows.at[t])
+
+    def key_copy(k):
+        to = (q + k) % R
+        return copy(keys_in.at[to], keys.at[y, q], s_keys.at[k - 1], r_keys.at[k - 1], to, s)
 
     def top_copy(k):
         to = (q + k) % R
         return copy(top_in.at[to], trcv.at[k - 1], s_top.at[k - 1], r_top.at[k - 1], to, s)
 
-    for k in range(1, R):
-        for c in rep_copies(k):
-            c.start()
-    mine = pltpu.make_async_copy(rows_in.at[q], rows.at[y, q], l_sem.at[0])
-    mine.start()
-    mine_keys = pltpu.make_async_copy(keys_in.at[q], keys.at[y, q], l_sem.at[1])
-    mine_keys.start()
+    own_keys = pltpu.make_async_copy(keys_in.at[q], keys.at[y, q], l_keys)
+    own_keys.start()
+    for k in range(1, R):
+        key_copy(k).start()
+
+    def send_rows(t):
+        own_row_copy(t).start()
+        for k in range(1, R):
+            row_copy(t, k).start()
+
+    each(0, T, send_rows)
     for k in range(1, R):
         top_copy(k).start()
-    mine.wait()
-    mine_keys.wait()
-
-    def pair_copies(k):
-        r = (q + R - k) % R
-        return (
-            copy(rows.at[y, r], rows.at[y, r], s_yrow.at[k], r_yrow.at[k], q, mate),
-            copy(keys.at[y, r], keys.at[y, r], s_ykey.at[k], r_ykey.at[k], q, mate),
-        )
-
-    for c in pair_copies(0):
-        c.start()
-    for k in range(1, R):
-        for c in rep_copies(k):
-            c.wait_recv()
-        for c in pair_copies(k):
-            c.start()
-
-    for k in range(1, R):
-        top_copy(k).wait_recv()
-    total = top_in[q].astype(f32)
-    for k in range(1, R):
-        total = total + trcv[k - 1].astype(f32)
-    tsum[...] = total.astype(bf16).reshape(tsum.shape)
-
-    def t2_copy(k):
-        to = (s + k) % S
-        return copy(tsum.at[to], tred.at[k - 1], s_t2.at[k - 1], r_t2.at[k - 1], q, to)
-
-    def t3_copy(k):
-        to = (s + k) % S
-        return copy(tfin, tgat.at[s], s_t3.at[k - 1], r_t3.at[k - 1], q, to)
-
-    def each(n, f):
-        def step(k, _):
-            f(k)
-            return 0
-
-        lax.fori_loop(1, n, step, 0)
-
-    each(S, lambda k: t2_copy(k).start())
-
-    for k in range(R):
-        for c in pair_copies(k):
-            c.wait_recv()
+
+    def pair_copy(t):
+        return copy(rows.at[y, t], rows.at[y, t], s_yrow.at[t], r_yrow.at[t], q, mate)
+
+    def pair_keys():
+        return copy(keys.at[y], keys.at[y], s_ykey, r_ykey, q, mate)
+
+    def stage_b(t):
+        for k in range(1, R):
+            row_copy(t, k).wait_recv()
+        own_row_copy(t).wait()
+        pair_copy(t).start()
 
     levels = lax.broadcasted_iota(jnp.int32, (span, B), 0)
 
@@ -192,75 +173,126 @@
                     key = keys[side, r, pl.ds(t * lookups + l, 1), :] - shard * span
                     hit = jnp.where(levels == key, 1.0, 0.0)
                     hits = hit if hits is None else hits + hit
-                acc = acc + jnp.dot(hits.astype(bf16), rows[side, r, t], preferred_element_type=f32)
+                acc = acc + jnp.dot(hits.astype(bf16), rows[side, t, r], preferred_element_type=f32)
         return acc
 
-    def part_copy(k):
+    def part_copy(t, k):
         to = ((z + k) % Z) * PAIR + y
-        return copy(part.at[k - 1], prcv.at[k - 1], s_part.at[k - 1], r_part.at[k - 1], q, to)
-
-    def send_part(k):
-        to = ((z + k) % Z) * PAIR + y
-
-        def table(t, _):
-            part[k - 1, t] = partial_of(t, to).astype(bf16)
-            return 0
-
-        lax.fori_loop(0, T, table, 0)
-        part_copy(k).start()
-
-    each(Z, send_part)
-
-    each(S, lambda k: t2_copy(k).wait_recv())
-    tfin[...] = lax.fori_loop(
-        1, S, lambda k, a: a + tred[k - 1].astype(f32), tsum[s].astype(f32)
-    ).astype(bf16)
-    each(S, lambda k: t3_copy(k).start())
-
-    def own_table(t, _):
+        return copy(part.at[t, k - 1], prcv.at[t, k - 1], s_part.at[t, k - 1], r_part.at[t, k - 1], q, to)
+
+    def stage_c(t):
+        pair_copy(t).wait_recv()
+
+        def send_part(k):
+            part[t, k - 1] = partial_of(t, ((z + k) % Z) * PAIR + y).astype(bf16)
+            part_copy(t, k).start()
+
+        each(1, Z, send_part)
         own[t] = partial_of(t, s)
+
+    def fin_copy(t, k):
+        to = twin if k == 0 else (q + CORES * k) % R
+        return copy(tab_out.at[q, t], tab_out.at[q, t], s_fin.at[t, k], r_fin.at[t, k], to, s)
+
+    def fin_forward(t, k):
+        origin = (q + R - CORES * k) % R
+        return copy(tab_out.at[origin, t], tab_out.at[origin, t], s_fwd.at[t, k - 1], r_fwd.at[t, k - 1], twin, s)
+
+    def stage_d(t):
+        each(1, Z, lambda k: part_copy(t, k).wait_recv())
+        tab_out[q, t] = lax.fori_loop(
+            1, Z, lambda k, a: a + prcv[t, k - 1].astype(f32), own[t]
+        ).astype(bf16)
+        for k in reversed(range(X)):
+            fin_copy(t, k).start()
+
+    def stage_e(t):
+        for k in range(1, X):
+            fin_copy(t, k).wait_recv()
+            fin_forward(t, k).start()
+
+    def t2_copy(k):
+        to = (s + k) % S
+        return copy(tsum.at[to], tred.at[k - 1], s_t2.at[k - 1], r_t2.at[k - 1], q, to)
+
+    def t3_copy(k):
+        to = (s + k) % S
+        return copy(tfin, top_out.at[q, s], s_t3.at[k - 1], r_t3.at[k - 1], q, to)
+
+    def t4_copy(k):
+        to = twin if k == 0 else (q + CORES * k) % R
+        return copy(top_out.at[q], top_out.at[q], s_t4.at[k], r_t4.at[k], to, s)
+
+    def t5_copy(k):
+        origin = (q + R - CORES * k) % R
+        return copy(top_out.at[origin], top_out.at[origin], s_t5.at[k - 1], r_t5.at[k - 1], twin, s)
+
+    def top_a():
+        total = top_in[q].astype(f32)
+        for k in range(1, R):
+            top_copy(k).wait_recv()
+            total = total + trcv[k - 1].astype(f32)
+        tsum[...] = total.astype(bf16)
+        each(1, S, lambda k: t2_copy(k).start())
+
+    def top_b():
+        each(1, S, lambda k: t2_copy(k).wait_recv())
+        tfin[...] = lax.fori_loop(
+            1, S, lambda k, a: a + tred[k - 1].astype(f32), tsum[s].astype(f32)
+        ).astype(bf16)
+        top_out[q, s] = tfin[...]
+        each(1, S, lambda k: t3_copy(k).start())
+
+    def top_c():
+        each(1, S, lambda k: t3_copy(k).wait_recv())
+        for k in reversed(range(X)):
+            t4_copy(k).start()
+
+    def top_d():
+        for k in range(1, X):
+            t4_copy(k).wait_recv()
+            t5_copy(k).start()
+
+    own_keys.wait()
+    for k in range(1, R):
+        key_copy(k).wait_recv()
+    pair_keys().start()
+    for t in range(min(2, T)):
+        stage_b(t)
+    pair_keys().wait_recv()
+
+    def step(i, _):
+        pl.when(i + 2 < T)(lambda: stage_b(i + 2))
+        pl.when(i < T)(lambda: stage_c(i))
+        for at, f in ((2, top_a), (4, top_b), (5, top_c), (7, top_d)):
+            pl.when(i == at)(f)
+        pl.when((i >= 2) & (i < T + 2))(lambda: stage_d(i - 2))
+        pl.when((i >= 3) & (i < T + 3))(lambda: stage_e(i - 3))
         return 0
 
-    lax.fori_loop(0, T, own_table, 0)
-    tgat[s] = tfin[...]
-    each(S, lambda k: t3_copy(k).wait_recv())
-
-    def t4_copy(k):
-        to = (q + k) % R
-        return copy(tgat, top_out.at[q], s_t4.at[k - 1], r_t4.at[k - 1], to, s)
-
-    def fin_copy(k):
-        to = (q + k) % R
-        return copy(fin, tab_out.at[q], s_fin.at[k - 1], r_fin.at[k - 1], to, s)
-
-    for k in range(1, R):
-        t4_copy(k).start()
-    each(Z, lambda k: part_copy(k).wait_recv())
-
-    def finish(t, _):
-        fin[t] = lax.fori_loop(
-            1, Z, lambda k, a: a + prcv[k - 1, t].astype(f32), own[t]
-        ).astype(bf16)
-        return 0
-
-    lax.fori_loop(0, T, finish, 0)
-    for k in range(1, R):
-        fin_copy(k).start()
-    top_out[q] = tgat[...]
-    tab_out[q] = fin[...]
-    for k in range(1, R):
-        for c in rep_copies(k):
-            c.wait_send()
+    lax.fori_loop(0, max(T + 3, 8), step, 0)
+
+    def drain(t):
+        for k in range(1, R):
+            row_copy(t, k).wait_send()
+        pair_copy(t).wait_send()
+        each(1, Z, lambda k: part_copy(t, k).wait_send())
+        fin_copy(t, 0).wait()
+        for k in range(1, X):
+            fin_copy(t, k).wait_send()
+            fin_forward(t, k).wait()
+
+    each(0, T, drain)
+    for k in range(1, R):
+        key_copy(k).wait_send()
         top_copy(k).wait_send()
-    for k in range(R):
-        for c in pair_copies(k):
-            c.wait_send()
-    each(S, lambda k: t2_copy(k).wait_send())
-    each(S, lambda k: t3_copy(k).wait_send())
-    each(Z, lambda k: part_copy(k).wait_send())
-    for k in range(1, R):
-        t4_copy(k).wait()
-        fin_copy(k).wait()
+    pair_keys().wait_send()
+    each(1, S, lambda k: t2_copy(k).wait_send())
+    each(1, S, lambda k: t3_copy(k).wait_send())
+    t4_copy(0).wait()
+    for k in range(1, X):
+        t4_copy(k).wait_send()
+        t5_copy(k).wait()
 
 
 def on_device(span, R, S, dense_out, pooled, top_weight, top_cotangent, indices):
@@ -300,7 +332,7 @@
     key_rows = cdiv(T * lookups, 8) * 8
     keys = jnp.pad(keys, ((0, 0), (0, key_rows - T * lookups), (0, 0)), constant_values=-1)
 
-    Z = S // PAIR
+    Z, X = S // PAIR, R // CORES
     dma = pltpu.SemaphoreType.DMA
     table_all, top_all = pl.pallas_call(
         functools.partial(comm_kernel, R, S, lookups),
@@ -311,22 +343,18 @@
         in_specs=[VMEM] * 3,
         out_specs=(VMEM,) * 2,
         scratch_shapes=[
-            pltpu.VMEM((PAIR, R, T, samples, emb), bf16),
+            pltpu.VMEM((PAIR, T, R, samples, emb), bf16),
             pltpu.VMEM((PAIR, R, key_rows, samples), jnp.int32),
-            pltpu.VMEM((Z - 1, T, span, emb), bf16),
-            pltpu.VMEM((Z - 1, T, span, emb), bf16),
+            pltpu.VMEM((T, Z - 1, span, emb), bf16),
+            pltpu.VMEM((T, Z - 1, span, emb), bf16),
             pltpu.VMEM((T, span, emb), f32),
-            pltpu.VMEM((T, span, emb), bf16),
             pltpu.VMEM((R - 1, S, chunk_rows, width), bf16),
             pltpu.VMEM((S, chunk_rows, width), bf16),
             pltpu.VMEM((S - 1, chunk_rows, width), bf16),
             pltpu.VMEM((chunk_rows, width), bf16),
-            pltpu.VMEM((S, chunk_rows, width), bf16),
-            dma((R - 1,)), dma((R - 1,)), dma((R - 1,)), dma((R - 1,)), dma((R - 1,)), dma((R - 1,)),
-            dma((R,)), dma((R,)), dma((R,)), dma((R,)),
-            dma((Z - 1,)), dma((Z - 1,)), dma((R - 1,)), dma((R - 1,)),
-            dma((S - 1,)), dma((S - 1,)), dma((S - 1,)), dma((S - 1,)),
-            dma((R - 1,)), dma((R - 1,)), dma((2,)),
+            *[dma((T, R - 1))] * 2, *[dma((R - 1,))] * 4, *[dma((T,))] * 2, dma, dma,
+            *[dma((T, Z - 1))] * 2, *[dma((T, X))] * 2, *[dma((T, X - 1))] * 2,
+            *[dma((S - 1,))] * 4, *[dma((X,))] * 2, *[dma((X - 1,))] * 2, dma((T,)), dma,
         ],
         compiler_params=pltpu.CompilerParams(
             collective_id=0, has_side_effects=True, vmem_limit_bytes=60 << 20

time: 147 us -> 111 us (0.76); the launches traced: 145 us -> 111 us
  Pallas kernels: 129 us -> 94.7 us
    pallas_call x1, Pallas kernels: 112 us -> 78 us  [on_device(): pl.pallas_call(functools.partial(comm_kernel, R, S, lookups), out_shape=(...]
where the time goes in v2:
time: 111 us
  Pallas kernels  94.7 us (85%)
  local copies, waits for them, and re-layouts  10.7 us (10%)
  other arithmetic  4.81 us (4%)
    pallas_call x1, Pallas kernels, on_device(): pl.pallas_call(functools.partial(comm_kernel, R, S, lookups), out_shape=(...  78 us
    pallas_call x1, Pallas kernels, on_device(): pl.pallas_call(functools.partial(local_kernel, nv, 9, 32), out_shape=(jax...  16.7 us
    unnamed x16, local copies, waits for them, and re-layouts  8.02 us

profile of v2, /device:TPU:0, one launch (start us, length us, event | category | flops | bytes accessed | tf_op | source)
XLA Modules:
  0.0 110.9 jit_solution(16131537068801805065)
XLA Ops:
  0.6 0.8 pad.8
  1.4 0.6 pad.9.keys_in
  2.0 0.0 copy-start.1
  2.0 1.2 %copy-done.1 = bf16[479,1024]{1,0:T(8,128)(2,1)S(1)} copy-done((bf16[479,1024]{1,0:T(8,128)(2,1)S(1)}, bf16[479,1024]{1,0:T(8,128)(2,1)}, u32[]{:S(2)}) %copy-start.1) | copy-done | bytes 981016
  3.2 0.0 copy-start.3
  3.2 1.2 %copy-done.3 = bf16[128,26,128]{2,0,1:T(8,128)(2,1)S(1)} copy-done((bf16[128,26,128]{2,0,1:T(8,128)(2,1)S(1)}, bf16[128,26,128]{2,0,1:T(8,128)(2,1)}, u32[]{:S(2)}) %copy-start.3) | copy-done | bytes 851992
  4.4 0.0 copy-start.4
  4.4 0.9 copy-done.4
  5.3 0.0 copy-start.5
  5.3 0.8 copy-done.5
  6.1 16.7 %local_math.1 = (bf16[128,128]{1,0:T(8,128)(2,1)}, bf16[28,128,128]{2,1,0:T(8,128)(2,1)S(1)}, bf16[4,512,256]{2,1,0:T(8,128)(2,1)S(1)}) custom-call(bf16[128,128]{1,0:T(8,128)(2,1)S(1)} %copy-done.5, bf16[26,128,128]{2,1,0:T(8,128)(2,1)S(1)} %bitcast.14, bf16[479,1024]{1,0:T(8,128)(2,1)S(1)} %copy-done.1, bf16[128,1024]{1,0:T(8,128)(2,1)S(1)} %copy-done.4), custom_call_target="tpu_custom_call" | custom-call | tf_op jit(solution)/shard_map/local_math/pallas_call | solution.py:308
  22.8 0.0 copy-start
  22.8 1.0 copy-done
  23.8 0.0 copy-start.2
  23.8 0.9 copy-done.2
  24.7 78.0 %exchange.1 = (bf16[4,7,256,128]{3,2,1,0:T(8,128)(2,1)}, bf16[4,8,64,256]{3,2,1,0:T(8,128)(2,1)}) custom-call(bf16[4,7,128,128]{3,2,1,0:T(8,128)(2,1)} %bitcast.13, s32[4,16,128]{2,1,0:T(8,128)} %pad.9.keys_in, bf16[4,8,64,256]{3,2,1,0:T(8,128)(2,1)} %bitcast.12), custom_call_target="tpu_custom_call" | custom-call | tf_op jit(solution)/shard_map/exchange/pallas_call | solution.py:337
  102.7 1.3 %slice_convert_fusion.2 = f32[1,4,256]{2,0,1:T(1,128)} fusion(bf16[512,4,256]{2,0,1:T(8,128)(2,1)} %bitcast.18), kind=kLoop, calls=%fused_computation.2 | loop fusion | flops 1024 | bytes 6144 | tf_op jit(solution)/shard_map/convert_element_type | solution.py:367
  104.1 1.4 %slice_convert_fusion.1 = f32[479,4,256]{2,0,1:T(8,128)S(1)} fusion(bf16[512,4,256]{2,0,1:T(8,128)(2,1)} %bitcast.19), kind=kLoop, calls=%fused_computation.1 | loop fusion | flops 490496 | bytes 2942976 | tf_op jit(solution)/shard_map/convert_element_type | solution.py:366
  105.4 1.3 %copy.10 = f32[479,4,256]{2,1,0:T(4,128)S(1)} copy(f32[479,4,256]{2,0,1:T(8,128)S(1)} %slice_convert_fusion.1) | data formatting | bytes 3923968 | tf_op jit(solution)/shard_map/convert_element_type | solution.py:366
  106.7 0.3 pad.10
  107.0 0.0 copy-start.6
  107.1 1.7 %copy.11 = f32[60,8,4,256]{3,1,2,0:T(8,128)} copy(f32[60,8,4,256]{3,2,1,0:T(4,128)S(1)} %bitcast.15) | data formatting | bytes 3932160
  108.8 0.0 copy-done.6
  108.8 2.1 %slice_convert_fusion = f32[26,256,128]{2,1,0:T(8,128)} fusion(bf16[28,256,128]{2,1,0:T(8,128)(2,1)S(1)} %bitcast.17), kind=kLoop, calls=%fused_computation | loop fusion | flops 851968 | bytes 5111808 | tf_op jit(solution)/shard_map/convert_element_type | solution.py:364
  (1 shorter events, 0.0 us)
Async XLA Ops:
  2.0 1.2 %copy-start.1 = (bf16[479,1024]{1,0:T(8,128)(2,1)S(1)}, bf16[479,1024]{1,0:T(8,128)(2,1)}, u32[]{:S(2)}) copy-start(bf16[479,1024]{1,0:T(8,128)(2,1)} %weight.1) | copy-start | bytes 2942980
  3.2 1.2 %copy-start.3 = (bf16[128,26,128]{2,0,1:T(8,128)(2,1)S(1)}, bf16[128,26,128]{2,0,1:T(8,128)(2,1)}, u32[]{:S(2)}) copy-start(bf16[128,26,128]{2,0,1:T(8,128)(2,1)} %param.6) | copy-start | bytes 2555908
  4.4 0.9 copy-start.4
  5.3 0.8 copy-start.5
  22.8 1.0 copy-start
  23.8 0.9 copy-start.2
  107.0 1.7 %copy-start.6 = (bf16[4,7,256,128]{3,2,1,0:T(8,128)(2,1)S(1)}, bf16[4,7,256,128]{3,2,1,0:T(8,128)(2,1)}, u32[]{:S(2)}) copy-start(bf16[4,7,256,128]{3,2,1,0:T(8,128)(2,1)} %get-tuple-element.13) | copy-start | bytes 5505028

commit v3 on v2

--- a/solution.py
+++ b/solution.py
@@ -176,19 +176,42 @@
                 acc = acc + jnp.dot(hits.astype(bf16), rows[side, t, r], preferred_element_type=f32)
         return acc
 
-    def part_copy(t, k):
-        to = ((z + k) % Z) * PAIR + y
-        return copy(part.at[t, k - 1], prcv.at[t, k - 1], s_part.at[t, k - 1], r_part.at[t, k - 1], q, to)
+    def up_copy(t, d):
+        to = ((z + 1) % Z) * PAIR + y
+        return copy(part.at[t, d], prcv.at[t, d + 1], s_part.at[t, d], r_part.at[t, d + 1], q, to)
+
+    def down_copy(t, d):
+        to = ((z + Z - 1) % Z) * PAIR + y
+        return copy(part.at[t, d], prcv.at[t, d], s_part.at[t, d], r_part.at[t, d], q, to)
 
     def stage_c(t):
         pair_copy(t).wait_recv()
 
-        def send_part(k):
-            part[t, k - 1] = partial_of(t, ((z + k) % Z) * PAIR + y).astype(bf16)
-            part_copy(t, k).start()
-
-        each(1, Z, send_part)
+        def up(d):
+            part[t, d] = partial_of(t, d * PAIR + y).astype(bf16)
+            pl.when(z == 0)(lambda: up_copy(t, d).start())
+
+        def down(d):
+            part[t, d] = partial_of(t, d * PAIR + y).astype(bf16)
+            pl.when(z == Z - 1)(lambda: down_copy(t, d).start())
+
+        each(z + 1, Z, up)
+        each(0, z, down)
         own[t] = partial_of(t, s)
+
+    def stage_pass(t):
+        def up(d):
+            up_copy(t, d).wait_recv()
+            part[t, d] = (part[t, d].astype(f32) + prcv[t, d + 1].astype(f32)).astype(bf16)
+            up_copy(t, d).start()
+
+        def down(d):
+            down_copy(t, d).wait_recv()
+            part[t, d] = (part[t, d].astype(f32) + prcv[t, d].astype(f32)).astype(bf16)
+            down_copy(t, d).start()
+
+        pl.when(z > 0)(lambda: each(z + 1, Z, up))
+        pl.when(z < Z - 1)(lambda: each(0, z, down))
 
     def fin_copy(t, k):
         to = twin if k == 0 else (q + CORES * k) % R
@@ -199,10 +222,17 @@
         return copy(tab_out.at[origin, t], tab_out.at[origin, t], s_fwd.at[t, k - 1], r_fwd.at[t, k - 1], twin, s)
 
     def stage_d(t):
-        each(1, Z, lambda k: part_copy(t, k).wait_recv())
-        tab_out[q, t] = lax.fori_loop(
-            1, Z, lambda k, a: a + prcv[t, k - 1].astype(f32), own[t]
-        ).astype(bf16)
+        def from_below():
+            up_copy(t, z).wait_recv()
+            own[t] = own[t] + prcv[t, z + 1].astype(f32)
+
+        def from_above():
+            down_copy(t, z).wait_recv()
+            own[t] = own[t] + prcv[t, z].astype(f32)
+
+        pl.when(z > 0)(from_below)
+        pl.when(z < Z - 1)(from_above)
+        tab_out[q, t] = own[t].astype(bf16)
         for k in reversed(range(X)):
             fin_copy(t, k).start()
 
@@ -266,17 +296,19 @@
         pl.when(i < T)(lambda: stage_c(i))
         for at, f in ((2, top_a), (4, top_b), (5, top_c), (7, top_d)):
             pl.when(i == at)(f)
-        pl.when((i >= 2) & (i < T + 2))(lambda: stage_d(i - 2))
-        pl.when((i >= 3) & (i < T + 3))(lambda: stage_e(i - 3))
+        pl.when((i >= 1) & (i < T + 1))(lambda: stage_pass(i - 1))
+        pl.when((i >= 3) & (i < T + 3))(lambda: stage_d(i - 3))
+        pl.when((i >= 4) & (i < T + 4))(lambda: stage_e(i - 4))
         return 0
 
-    lax.fori_loop(0, max(T + 3, 8), step, 0)
+    lax.fori_loop(0, max(T + 4, 8), step, 0)
 
     def drain(t):
         for k in range(1, R):
             row_copy(t, k).wait_send()
         pair_copy(t).wait_send()
-        each(1, Z, lambda k: part_copy(t, k).wait_send())
+        each(z + 1, Z, lambda d: up_copy(t, d).wait_send())
+        each(0, z, lambda d: down_copy(t, d).wait_send())
         fin_copy(t, 0).wait()
         for k in range(1, X):
             fin_copy(t, k).wait_send()
@@ -293,6 +325,19 @@
     for k in range(1, X):
         t4_copy(k).wait_send()
         t5_copy(k).wait()
+
+
+def finish_kernel(table_in, top_in, table_out, top_out, bias_out):
+    def table(t, _):
+        table_out[t] = table_in[t].astype(f32)
+        return 0
+
+    lax.fori_loop(0, table_out.shape[0], table, 0)
+    features, width = top_out.shape[0], top_in.shape[2]
+    for r in range(top_in.shape[0]):
+        block = top_in[r, pl.ds(0, cdiv(features + 1, 16) * 16), :].astype(f32)
+        top_out[:, pl.ds(r * width, width)] = block[:features]
+        bias_out[:, pl.ds(r * width, width)] = block[features : features + 1]
 
 
 def on_device(span, R, S, dense_out, pooled, top_weight, top_cotangent, indices):
@@ -345,15 +390,15 @@
         scratch_shapes=[
             pltpu.VMEM((PAIR, T, R, samples, emb), bf16),
             pltpu.VMEM((PAIR, R, key_rows, samples), jnp.int32),
-            pltpu.VMEM((T, Z - 1, span, emb), bf16),
-            pltpu.VMEM((T, Z - 1, span, emb), bf16),
+            pltpu.VMEM((T, Z, span, emb), bf16),
+            pltpu.VMEM((T, Z + 1, span, emb), bf16),
             pltpu.VMEM((T, span, emb), f32),
             pltpu.VMEM((R - 1, S, chunk_rows, width), bf16),
             pltpu.VMEM((S, chunk_rows, width), bf16),
             pltpu.VMEM((S - 1, chunk_rows, width), bf16),
             pltpu.VMEM((chunk_rows, width), bf16),
             *[dma((T, R - 1))] * 2, *[dma((R - 1,))] * 4, *[dma((T,))] * 2, dma, dma,
-            *[dma((T, Z - 1))] * 2, *[dma((T, X))] * 2, *[dma((T, X - 1))] * 2,
+            dma((T, Z)), dma((T, Z + 1)), *[dma((T, X))] * 2, *[dma((T, X - 1))] * 2,
             *[dma((S - 1,))] * 4, *[dma((X,))] * 2, *[dma((X - 1,))] * 2, dma((T,)), dma,
         ],
         compiler_params=pltpu.CompilerParams(
@@ -361,10 +406,19 @@
         ),
         name="exchange",
     )(rows.reshape(R, T, samples, emb), keys, top.reshape(R, S, chunk_rows, width))
-    table_grad = table_all.reshape(R * T, span, emb)[:tables].astype(f32)
-    whole = jnp.transpose(top_all.reshape(R, height, width), (1, 0, 2)).reshape(height, hidden)
-    top_grad = whole[:features].astype(f32)
-    bias_grad = whole[features].astype(f32)
+    table_grad, top_grad, bias = pl.pallas_call(
+        finish_kernel,
+        out_shape=(
+            jax.ShapeDtypeStruct((tables, span, emb), f32),
+            jax.ShapeDtypeStruct((features, hidden), f32),
+            jax.ShapeDtypeStruct((1, hidden), f32),
+        ),
+        in_specs=[VMEM] * 2,
+        out_specs=(VMEM,) * 3,
+        compiler_params=pltpu.CompilerParams(vmem_limit_bytes=48 << 20),
+        name="finish",
+    )(table_all.reshape(R * T, span, emb), top_all.reshape(R, height, width))
+    bias_grad = bias.reshape(hidden)
     return dense_grad, top_grad, bias_grad, table_grad
 
 

time: 111 us -> 133 us (1.20)
  Pallas kernels: 94.7 us -> 122 us
  other arithmetic: 4.81 us -> 0 us
    pallas_call x1, Pallas kernels: 78 us -> 103 us  [on_device(): pl.pallas_call(functools.partial(comm_kernel, R, S, lookups), out_shape=(...]
    convert_element_type x3 -> x0, other arithmetic: 4.81 us -> none  [the longest x1 2.14 us: on_device(): table_grad = table_all.reshape(R * T, span, emb)[:tables].astype(f32)]
    pallas_call x0 -> x1, Pallas kernels: none -> 2.69 us  [on_device(): pl.pallas_call(finish_kernel, out_shape=(jax.ShapeDtypeStruct((tables, sp...]
where the time goes in v3:
time: 133 us
  Pallas kernels  122 us (92%)
  local copies, waits for them, and re-layouts  10.1 us (8%)
    pallas_call x1, Pallas kernels, on_device(): pl.pallas_call(functools.partial(comm_kernel, R, S, lookups), out_shape=(...  103 us
    pallas_call x1, Pallas kernels, on_device(): pl.pallas_call(functools.partial(local_kernel, nv, 9, 32), out_shape=(jax...  16.7 us
    unnamed x16, local copies, waits for them, and re-layouts  8.67 us
    pallas_call x1, Pallas kernels, on_device(): pl.pallas_call(finish_kernel, out_shape=(jax.ShapeDtypeStruct((tables, sp...  2.69 us

profile of v3, /device:TPU:0, one launch (start us, length us, event | category | flops | bytes accessed | tf_op | source)
XLA Modules:
  0.0 133.0 jit_solution(3251613488852315990)
XLA Ops:
  0.6 0.8 pad.8
  1.4 0.6 pad.9.keys_in
  2.0 0.0 copy-start.3
  2.0 1.2 copy-done.3
  3.2 0.0 copy-start.5
  3.2 1.2 copy-done.5
  4.4 0.0 copy-start.6
  4.4 0.9 copy-done.6
  5.3 0.0 copy-start.7
  5.4 0.8 copy-done.7
  6.1 16.7 %local_math.1 = (bf16[128,128]{1,0:T(8,128)(2,1)}, bf16[28,128,128]{2,1,0:T(8,128)(2,1)S(1)}, bf16[4,512,256]{2,1,0:T(8,128)(2,1)S(1)}) custom-call(bf16[128,128]{1,0:T(8,128)(2,1)S(1)} %copy-done.7, bf16[26,128,128]{2,1,0:T(8,128)(2,1)S(1)} %bitcast.11, bf16[479,1024]{1,0:T(8,128)(2,1)S(1)} %copy-done.3, bf16[128,1024]{1,0:T(8,128)(2,1)S(1)} %copy-done.6), custom_call_target="tpu_custom_call" | custom-call | tf_op jit(solution)/shard_map/local_math/pallas_call | solution.py:353
  22.8 0.0 copy-start.1
  22.8 1.0 copy-done.1
  23.8 0.0 copy-start.4
  23.8 0.9 copy-done.4
  24.7 102.8 %exchange.1 = (bf16[4,7,256,128]{3,2,1,0:T(8,128)(2,1)}, bf16[4,8,64,256]{3,2,1,0:T(8,128)(2,1)}) custom-call(bf16[4,7,128,128]{3,2,1,0:T(8,128)(2,1)} %bitcast.10, s32[4,16,128]{2,1,0:T(8,128)} %pad.9.keys_in, bf16[4,8,64,256]{3,2,1,0:T(8,128)(2,1)} %bitcast.8), custom_call_target="tpu_custom_call" | custom-call | tf_op jit(solution)/shard_map/exchange/pallas_call | solution.py:382
  127.6 0.0 copy-start
  127.6 1.5 %copy-done = bf16[4,7,256,128]{3,2,1,0:T(8,128)(2,1)S(1)} copy-done((bf16[4,7,256,128]{3,2,1,0:T(8,128)(2,1)S(1)}, bf16[4,7,256,128]{3,2,1,0:T(8,128)(2,1)}, u32[]{:S(2)}) %copy-start) | copy-done | bytes 1835032
  129.1 0.0 copy-start.2
  129.1 1.2 copy-done.2
  130.3 2.7 %finish.1 = (f32[26,256,128]{2,1,0:T(8,128)}, f32[479,1024]{1,0:T(8,128)}, f32[1,1024]{1,0:T(1,128)}) custom-call(bf16[28,256,128]{2,1,0:T(8,128)(2,1)S(1)} %bitcast.7, bf16[4,512,256]{2,1,0:T(8,128)(2,1)S(1)} %bitcast.9), custom_call_target="tpu_custom_call" | custom-call | tf_op jit(solution)/shard_map/finish/pallas_call | solution.py:409
  (1 shorter events, 0.0 us)
Async XLA Ops:
  2.0 1.2 copy-start.3
  3.2 1.2 copy-start.5
  4.4 0.9 copy-start.6
  5.3 0.8 copy-start.7
  22.8 1.0 copy-start.1
  23.8 0.9 copy-start.4
  127.6 1.5 %copy-start = (bf16[4,7,256,128]{3,2,1,0:T(8,128)(2,1)S(1)}, bf16[4,7,256,128]{3,2,1,0:T(8,128)(2,1)}, u32[]{:S(2)}) copy-start(bf16[4,7,256,128]{3,2,1,0:T(8,128)(2,1)} %get-tuple-element.15) | copy-start | bytes 5505028
  129.1 1.2 copy-start.2
